TPU v7x, 32 devices: a whole 2x2x4 slice. The times are simulated.
32 devices in a mesh: ctx: 4 (over z), tp: 8 (over y, x, core).
Axes of the slice: x: 2, y: 2, z: 4, core: 2. Of those that a mesh axis runs over, the one named last changes fastest.
Arguments:
- query_states: bfloat16 [1024, 8192], P('ctx', 'tp'), may hold values from -6 to 6
- key_states: bfloat16 [1024, 1024], P('ctx'), may hold values from -6 to 6
- value_states: bfloat16 [1024, 1024], P('ctx'), may hold values from -6 to 6
- out_weight: bfloat16 [8192, 8192], P('tp'), may hold values from -0.5 to 0.5
- span_order: int32 [8], replicated, may hold values from 0 to 7, as said below
Outputs:
- projected: bfloat16 [1024, 8192], P('ctx', 'tp')
- z_loss: float32 [], replicated
Inputs may be any that keep to these rules, and one draw needn't show every extreme that they name: span_order is a permutation of 0 to 7, and for every d the slots 2 d and 2 d + 1 hold spans c and 7 - c for some c.
All inputs are finite; a program needn't handle non-finite values.
Results may differ from a plain program's by a relative error of at most 0.0075.
Values may be sent and summed in bfloat16 or wider, within the bound.
A program may use at most 64 MiB of HBM per device.

v0:
```python
import math

import jax
import jax.numpy as jnp
from jax import lax
from jax.sharding import PartitionSpec as P

QH = 64
KVH = 8
HD = 128


z_coef = 0.01
neg_large = -1e30


def absorb(carried, query_rows, query_pos, key_piece, value_piece, key_pos):
    row_peak, normalizer, weighted = carried
    scores = lax.dot_general(
        query_rows, key_piece, (((1,), (1,)), ((), ())), preferred_element_type=jnp.float32
    ) * (1.0 / math.sqrt(HD))
    visible = key_pos[None, :] <= query_pos[:, None]
    block_peak = jnp.max(jnp.where(visible, scores, neg_large), axis=1)
    new_peak = jnp.maximum(row_peak, block_peak)
    exp_terms = jnp.where(visible, jnp.exp(scores - new_peak[:, None]), 0.0)
    normalizer = jnp.sum(exp_terms, axis=1)
    weighted = jnp.dot(
        exp_terms.astype(jnp.bfloat16), value_piece, preferred_element_type=jnp.float32
    )
    return (new_peak, normalizer, weighted)


def on_device(query_states, key_states, value_states, out_weight, span_order):
    head_count = query_states.shape[1] // HD
    group_size = QH // KVH
    span_rows = query_states.shape[0] // 2
    span_total = span_order.shape[0]
    kv_start = lax.axis_index("tp") * head_count // group_size * HD
    own_keys = lax.dynamic_slice_in_dim(key_states, kv_start, HD, 1)
    own_values = lax.dynamic_slice_in_dim(value_states, kv_start, HD, 1)

    def slot_positions(slot_rows):
        slot_ids = slot_rows // span_rows
        match_table = slot_ids[:, None] == jnp.arange(span_total, dtype=jnp.int32)[None, :]
        chosen = jnp.sum(jnp.where(match_table, span_order[None, :], 0), axis=1)
        return chosen * span_rows + slot_rows % span_rows

    local_rows = jnp.arange(2 * span_rows, dtype=jnp.int32) + 2 * span_rows * lax.axis_index("ctx")
    query_pos = slot_positions(local_rows).reshape(2, 1, span_rows)
    query_pos = jnp.broadcast_to(query_pos, (2, head_count, span_rows)).reshape(
        2, head_count * span_rows
    )
    query_halves = jnp.transpose(
        query_states.reshape(2, span_rows, head_count, HD), (0, 2, 1, 3)
    ).reshape(2, head_count * span_rows, HD)
    query_flat = query_halves.reshape(2 * head_count * span_rows, HD)
    query_pos_flat = query_pos.reshape(-1)
    initial = (
        jnp.full((2, head_count * span_rows), neg_large, jnp.float32),
        jnp.zeros((2, head_count * span_rows), jnp.float32),
        jnp.zeros((2, head_count * span_rows, HD), jnp.float32),
    )
    key_piece = lax.all_gather(own_keys, "ctx", axis=0, tiled=True)
    value_piece = lax.all_gather(own_values, "ctx", axis=0, tiled=True)
    key_pos = slot_positions(jnp.arange(key_piece.shape[0], dtype=jnp.int32))
    flattened = (initial[0].reshape(-1), initial[1].reshape(-1), initial[2].reshape(-1, HD))
    updated = absorb(flattened, query_flat, query_pos_flat, key_piece, value_piece, key_pos)
    row_peak = updated[0].reshape(initial[0].shape)
    normalizer = updated[1].reshape(initial[1].shape)
    weighted = updated[2].reshape(initial[2].shape)
    mixed = (weighted / normalizer[:, :, None]).astype(jnp.bfloat16)
    attended = jnp.transpose(mixed.reshape(2, head_count, span_rows, HD), (0, 2, 1, 3)).reshape(
        2 * span_rows, head_count * HD
    )
    log_norm = row_peak + jnp.log(normalizer)
    squares_total = lax.psum(jnp.sum(log_norm * log_norm), ("ctx", "tp"))
    z_loss = z_coef * squares_total / (QH * 2 * span_rows * lax.axis_size("ctx"))
    summed = lax.psum_scatter(
        lax.dot_general(
            out_weight, attended, (((0,), (1,)), ((), ())), preferred_element_type=jnp.float32
        ),
        "tp",
        scatter_dimension=0,
        tiled=True,
    )
    projected = jnp.transpose(summed).astype(jnp.bfloat16)
    return (projected, z_loss)


def solution(mesh):
    return jax.shard_map(
        on_device,
        mesh=mesh,
        in_specs=(P("ctx", "tp"), P("ctx", None), P("ctx", None), P("tp", None), P()),
        out_specs=(P("ctx", "tp"), P()),
        check_vma=False,
    )
```

profile of v0, /device:TPU:0, one launch (start us, length us, event | category | flops | bytes accessed | tf_op | source)
XLA Modules:
  0.0 144.6 jit_solution(17041459061739847915)
XLA Ops:
  7.2 0.0 copy-start
  7.2 0.0 reduce-scatter.2.cloned.1.call-start
  7.3 0.9 copy-done
  8.2 15.7 %all_gather.7 = bf16[1024,128]{1,0:T(8,128)(2,1)S(1)} all-gather(bf16[256,128]{1,0:T(8,128)(2,1)S(1)} %constant_dynamic-slice_fusion.1), channel_id=1, replica_groups=mesh['ctx'=4,'tp'=8] {'ctx'}, dimensions={0}, use_global_device_ids=true | all-gather | bytes 327680 | tf_op jit(solution)/shard_map/all_gather | solution.py:64
  23.9 0.7 select_reduce_fusion.1
  24.7 0.7 select_reduce_fusion
  25.4 0.9 constant_dynamic-slice_fusion
  26.3 14.4 %all_gather.6 = bf16[1024,128]{1,0:T(8,128)(2,1)S(1)} all-gather(bf16[256,128]{1,0:T(8,128)(2,1)S(1)} %constant_dynamic-slice_fusion), channel_id=1, replica_groups=mesh['ctx'=4,'tp'=8] {'ctx'}, dimensions={0}, use_global_device_ids=true | all-gather | bytes 327680 | tf_op jit(solution)/shard_map/all_gather | solution.py:63
  40.7 1.1 copy.14
  41.9 0.1 copy.11
  42.0 1.3 fusion
  43.3 2.4 %fusion.2 = f32[2048]{0:T(1024)S(1)} fusion(f32[1024,2048]{1,0:T(8,128)S(1)} %get-tuple-element.3, f32[2048]{0:T(1024)S(1)} %broadcast_maximum_fusion, s32[2048]{0:T(1024)S(1)} %broadcast_bitcast_fusion, s32[1024]{0:T(1024)S(1)} %fusion.16), kind=kLoop, calls=%fused_computation.6 | loop fusion | flops 10483712 | bytes 8417280 | tf_op jit(solution)/shard_map/reduce_sum | solution.py:26
  45.7 2.2 %fusion.4 = f32[2048,128]{1,0:T(8,128)S(1)} fusion(bf16[1024,128]{1,0:T(8,128)(2,1)S(1)} %all_gather.7, f32[1024,2048]{1,0:T(8,128)S(1)} %get-tuple-element.3, f32[2048]{0:T(1024)S(1)} %broadcast_maximum_fusion, s32[2048]{0:T(1024)S(1)} %broadcast_bitcast_fusion, s32[1024]{0:T(1024)S(1)} %fusion.16), kind=kOutput, calls=%fused_computation.8 | convolution fusion | flops 547356672 | bytes 9719808 | tf_op jit(solution)/shard_map/dot_general | solution.py:27
  47.9 0.1 copy.12
  48.1 0.7 fusion.7
  48.8 12.5 %convolution_bitcast_fusion = f32[8192,256]{0,1:T(8,128)} fusion(bf16[1024,8192]{1,0:T(8,128)(2,1)} %param.8, bf16[32,8,8,128]{3,2,1,0:T(8,128)(2,1)S(1)} %bitcast.40), kind=kOutput, calls=%fused_computation | convolution fusion | flops 4294967296 | bytes 25690112 | tf_op jit(solution)/shard_map/dot_general | solution.py:79
  61.3 0.0 reduce-scatter.2.cloned.1.call-update
  61.3 0.6 multiply_reduce_fusion
  61.9 40.9 %psum.7 = f32[]{:T(128)} all-reduce(f32[]{:T(128)} %multiply_reduce_fusion), channel_id=1, replica_groups=mesh['ctx'=4,'tp'=8] {'ctx','tp'}, use_global_device_ids=true, to_apply=%region_6.7 | all-reduce | flops 1 | bytes 8 | tf_op jit(solution)/shard_map/psum | solution.py:76
  103.5 31.0 %reduce-scatter.2.cloned.1.call-done = f32[1024,256]{0,1:T(8,128)} async-done(((f32[8192,256]{0,1:T(8,128)}), f32[1024,256]{0,1:T(8,128)}) %reduce-scatter.2.cloned.1.call-update) | async-done | bytes 1048592 | tf_op jit(solution)/shard_map/reduce_scatter | solution.py:78
  134.5 2.1 %convert_bitcast_fusion = bf16[256,1024]{1,0:T(8,128)(2,1)} fusion(f32[1024,256]{0,1:T(8,128)} %reduce-scatter.2.cloned.1.call-done), kind=kLoop, calls=%fused_computation.15 | loop fusion | flops 262144 | bytes 1572864 | tf_op jit(solution)/shard_map/convert_element_type | solution.py:86
  (8 shorter events, 0.1 us)
Async XLA Ops:
  7.2 1.0 copy-start
  7.2 127.3 %reduce-scatter.2.cloned.1.call-start = ((), (), s32[]{:S(2)}) async-start(), calls=%async_computation.1 | async-start | bytes 9437184 | tf_op jit(solution)/shard_map/reduce_scatter | solution.py:78
Sparse Core Ops, SparseCore 0:
  61.4 73.0 reduce-scatter.1
where the time goes:
time: 145 us
  blocking collectives  71 us (49%)
  waiting for transfers between devices  31 us (21%)
  matrix products  16 us (11%)
  between operations  15.9 us (11%)
  other arithmetic  7.33 us (5%)
  local copies, waits for them, and re-layouts  3.21 us (2%)
    psum x1, blocking collectives, on_device(): squares_total = lax.psum(jnp.sum(log_norm * log_norm), ('ctx', 'tp'))  40.9 us
    reduce_scatter x1, waiting for transfers between devices, on_device(): lax.psum_scatter(lax.dot_general(out_weight, attended, (((0,), (1,)), (()...  31 us
    all_gather x1, blocking collectives, on_device(): value_piece = lax.all_gather(own_values, 'ctx', axis=0, tiled=True)  15.7 us
    all_gather x1, blocking collectives, on_device(): key_piece = lax.all_gather(own_keys, 'ctx', axis=0, tiled=True)  14.4 us
    dot_general x1, matrix products, on_device(): lax.dot_general(out_weight, attended, (((0,), (1,)), ((), ())), preferred...  12.5 us
  transfers between devices with their start and end apart: 1, of which 1 were waited for; matrix products, arithmetic and copies ran while one was open for 0% of the time, Pallas kernels for 0%

commit v1 on v0

v1 whole, which is shorter than its diff:
```python
import functools
import math

import jax
import jax.numpy as jnp
from jax import lax
from jax.experimental import pallas as pl
from jax.experimental.pallas import tpu as pltpu
from jax.sharding import PartitionSpec as P

QH = 64
KVH = 8
HD = 128

z_coef = 0.01
neg_large = -1e30
MESH = pl.DeviceIdType.MESH
LOG2E = math.log2(math.e)
LN2 = math.log(2.0)


def chunk_plan(chunk, tp):
    bits = tp.bit_length() - 1
    rest = list(range(1, bits))
    order = [0] + (rest if chunk % 2 == 0 else rest[::-1])
    kept = list(range(tp))
    slots, sends, keeps = {}, [], []
    offset = 0
    for stage, bit in enumerate(order):
        send = [e for e in kept if (e >> bit) & 1]
        kept = [e for e in kept if not (e >> bit) & 1]
        for e in kept:
            slots[stage, e] = offset
            offset += 1
        sends.append(send)
        keeps.append(list(kept))
    return order, slots, sends, keeps


def kernel(
    n_ctx, tp, heads, chunks, count,
    so_ref, q_hbm, k_hbm, v_hbm, w_hbm, out_ref, z_ref,
    qbuf, kbuf, vbuf, wbuf, bias, att, acc, sbuf, rbuf, zctx, zsend, zrecv,
    local_sem, w_sem, kv_send, kv_recv, rs_send, rs_recv, zc_send, zc_recv, zt_send, zt_recv,
):
    z = lax.axis_index("ctx")
    t = lax.axis_index("tp")
    bits = tp.bit_length() - 1
    rows = qbuf.shape[0]
    span_rows = rows // 2
    width = wbuf.shape[-1]
    cols = width * chunks
    tbit = [lax.rem(lax.div(t, 1 << b), 2) for b in range(bits)]

    def owner(e):
        d = 0
        for b in range(bits):
            d = d + ((1 - tbit[b]) if (e >> b) & 1 else tbit[b]) * (1 << b)
        return d

    def partner(bit):
        return t + (1 - 2 * tbit[bit]) * (1 << bit)

    plans = [chunk_plan(c, tp) for c in range(chunks)]

    kv_start = pl.multiple_of(lax.div(t * heads, QH // KVH) * HD, HD)
    own = pl.ds(pl.multiple_of(z * rows, rows), rows)
    k_in = pltpu.make_async_copy(k_hbm.at[:, pl.ds(kv_start, HD)], kbuf.at[own, :], local_sem.at[0])
    v_in = pltpu.make_async_copy(v_hbm.at[:, pl.ds(kv_start, HD)], vbuf.at[own, :], local_sem.at[1])
    q_in = pltpu.make_async_copy(q_hbm, qbuf, local_sem.at[2])
    k_in.start()
    v_in.start()
    q_in.start()

    barrier = pltpu.get_barrier_semaphore()
    for r in range(1, n_ctx):
        pl.semaphore_signal(barrier, inc=1, device_id=(lax.rem(z + r, n_ctx), t), device_id_type=MESH)
    for b in range(bits):
        pl.semaphore_signal(barrier, inc=1, device_id=(z, partner(b)), device_id_type=MESH)

    w_in = {}
    for c in range(chunks):
        _, _, sends, keeps = plans[c]
        for e in sends[0] + keeps[0]:
            start = pl.multiple_of(owner(e) * cols + c * width, width)
            w_in[c, e] = pltpu.make_async_copy(
                w_hbm.at[:, pl.ds(start, width)], wbuf.at[c, e], w_sem.at[c, e]
            )
            w_in[c, e].start()
    pl.semaphore_wait(barrier, n_ctx - 1 + bits)

    def piece(which, j):
        return (kbuf, vbuf)[which].at[pl.ds(pl.multiple_of(j * rows, rows), rows), :]

    def kv_copy(d, dist, which):
        step = 1 - 2 * d
        ref = piece(which, z - step * dist)
        return pltpu.make_async_remote_copy(
            src_ref=ref, dst_ref=ref,
            send_sem=kv_send.at[d, dist, which], recv_sem=kv_recv.at[d, dist, which],
            device_id=(z + step, t), device_id_type=MESH,
        )

    def kv_arrival(d, dist, which):
        step = 1 - 2 * d
        ref = piece(which, z - step * dist)
        return pltpu.make_async_remote_copy(
            src_ref=ref, dst_ref=ref,
            send_sem=kv_send.at[d, dist - 1, which], recv_sem=kv_recv.at[d, dist - 1, which],
            device_id=(z + step, t), device_id_type=MESH,
        )

    def can_send(d, dist):
        if d == 0:
            return jnp.logical_and(z >= dist, z + 1 < n_ctx)
        return jnp.logical_and(z + dist < n_ctx, z >= 1)

    def has_source(d, dist):
        return z >= dist if d == 0 else z + dist < n_ctx

    for which in range(2):
        (k_in, v_in)[which].wait()
        for d in range(2):
            @pl.when(can_send(d, 0))
            def _(d=d, which=which):
                kv_copy(d, 0, which).start()

    for half in range(2):
        q_pos = so_ref[2 * z + half] * span_rows + lax.broadcasted_iota(jnp.int32, (span_rows, span_rows), 0)
        for s in range(2 * n_ctx):
            k_pos = so_ref[s] * span_rows + lax.broadcasted_iota(jnp.int32, (span_rows, span_rows), 1)
            bias[half * span_rows:(half + 1) * span_rows, s * span_rows:(s + 1) * span_rows] = jnp.where(
                k_pos <= q_pos, 0.0, neg_large
            )
    q_in.wait()

    for dist in range(1, n_ctx):
        for which in range(2):
            for d in range(2):
                @pl.when(has_source(d, dist))
                def _(d=d, which=which, dist=dist):
                    kv_arrival(d, dist, which).wait_recv()

                @pl.when(can_send(d, dist))
                def _(d=d, which=which, dist=dist):
                    kv_copy(d, dist, which).start()

    def one_head(h, squares):
        lanes = pl.ds(pl.multiple_of(h * HD, HD), HD)
        scores = lax.dot_general(
            qbuf[:, lanes], kbuf[...], (((1,), (1,)), ((), ())), preferred_element_type=jnp.float32
        ) * (LOG2E / math.sqrt(HD)) + bias[...]
        peak = jnp.max(scores, axis=1, keepdims=True)
        terms = jnp.exp2(scores - peak)
        normalizer = jnp.sum(terms, axis=1, keepdims=True)
        weighted = jnp.dot(terms.astype(jnp.bfloat16), vbuf[...], preferred_element_type=jnp.float32)
        att[:, lanes] = (weighted / normalizer).astype(jnp.bfloat16)
        log_norm = peak * LN2 + jnp.log(normalizer)
        return squares + log_norm * log_norm

    squares = lax.fori_loop(0, heads, one_head, jnp.zeros((rows, 1), jnp.float32))
    zctx[0] = jnp.broadcast_to(jnp.sum(squares, axis=0, keepdims=True), zctx.shape[1:])

    def zc_copy(r):
        return pltpu.make_async_remote_copy(
            src_ref=zctx.at[0], dst_ref=zctx.at[r], send_sem=zc_send.at[r], recv_sem=zc_recv.at[r],
            device_id=(lax.rem(z + r, n_ctx), t), device_id_type=MESH,
        )

    for r in range(1, n_ctx):
        zc_copy(r).start()

    def rs_copy(c, stage, e_kept):
        order, slots, _, _ = plans[c]
        slot = slots[stage, e_kept]
        return pltpu.make_async_remote_copy(
            src_ref=sbuf.at[c, slot], dst_ref=rbuf.at[c, slot],
            send_sem=rs_send.at[c, slot], recv_sem=rs_recv.at[c, slot],
            device_id=(z, partner(order[stage])), device_id_type=MESH,
        )

    def push(c, stage, e, value):
        order, slots, _, _ = plans[c]
        e_kept = e ^ (1 << order[stage])
        sbuf[c, slots[stage, e_kept]] = value.astype(jnp.bfloat16)
        rs_copy(c, stage, e_kept).start()

    def project(c):
        _, slots, sends, keeps = plans[c]
        for e in sends[0]:
            w_in[c, e].wait()
            push(c, 0, e, jnp.dot(att[...], wbuf[c, e], preferred_element_type=jnp.float32))
        for e in keeps[0]:
            w_in[c, e].wait()
            acc[c, slots[0, e]] = jnp.dot(att[...], wbuf[c, e], preferred_element_type=jnp.float32)

    def combine(c, stage):
        order, slots, sends, keeps = plans[c]
        later = sends[stage + 1] + keeps[stage + 1] if stage + 1 < bits else [0]
        for e in later:
            rs_copy(c, stage, e).wait_recv()
            value = acc[c, slots[0, e]] + rbuf[c, slots[stage, e]].astype(jnp.float32)
            if stage + 1 == bits:
                out_ref[:, c * width:(c + 1) * width] = value.astype(jnp.bfloat16)
            elif e in sends[stage + 1]:
                push(c, stage + 1, e, value)
            else:
                acc[c, slots[0, e]] = value

    for c in range(chunks):
        project(c)
        if c >= 1:
            combine(c - 1, 0)
    combine(chunks - 1, 0)

    for r in range(1, n_ctx):
        zc_copy(r).wait_recv()
    total = zctx[lax.rem(z, n_ctx)]
    for j in range(1, n_ctx):
        total = total + zctx[lax.rem(z - j + n_ctx, n_ctx)]

    def zt_copy(b):
        return pltpu.make_async_remote_copy(
            src_ref=zsend.at[b], dst_ref=zrecv.at[b], send_sem=zt_send.at[b], recv_sem=zt_recv.at[b],
            device_id=(z, partner(b)), device_id_type=MESH,
        )

    for b in range(bits):
        zsend[b] = total
        zt_copy(b).start()
        if b + 1 < bits:
            for c in range(chunks):
                combine(c, b + 1)
        zt_copy(b).wait_recv()
        total = total + zrecv[b]
    z_ref[...] = total[0:1, 0:1] * (z_coef / count)

    for which in range(2):
        for d in range(2):
            for dist in range(n_ctx - 1):
                @pl.when(can_send(d, dist))
                def _(d=d, which=which, dist=dist):
                    kv_copy(d, dist, which).wait_send()
    for r in range(1, n_ctx):
        zc_copy(r).wait_send()
    for b in range(bits):
        zt_copy(b).wait_send()
    for c in range(chunks):
        order, slots, _, keeps = plans[c]
        for stage in range(bits):
            for e in keeps[stage]:
                rs_copy(c, stage, e).wait_send()


def on_device(n_ctx, tp, query_states, key_states, value_states, out_weight, span_order):
    rows, q_cols = query_states.shape
    heads = q_cols // HD
    depth, model = out_weight.shape
    cols = model // tp
    width = min(256, cols)
    chunks = cols // width
    bits = tp.bit_length() - 1
    tokens = rows * n_ctx
    any_spec = pl.BlockSpec(memory_space=pl.ANY)
    vmem_spec = pl.BlockSpec(memory_space=pltpu.VMEM)
    dma = pltpu.SemaphoreType.DMA
    projected, z_loss = pl.pallas_call(
        functools.partial(kernel, n_ctx, tp, heads, chunks, QH * tokens),
        out_shape=(
            jax.ShapeDtypeStruct((rows, cols), jnp.bfloat16),
            jax.ShapeDtypeStruct((1, 1), jnp.float32),
        ),
        in_specs=[pl.BlockSpec(memory_space=pltpu.SMEM)] + [any_spec] * 4,
        out_specs=(vmem_spec, vmem_spec),
        scratch_shapes=[
            pltpu.VMEM((rows, q_cols), jnp.bfloat16),
            pltpu.VMEM((tokens, HD), jnp.bfloat16),
            pltpu.VMEM((tokens, HD), jnp.bfloat16),
            pltpu.VMEM((chunks, tp, depth, width), jnp.bfloat16),
            pltpu.VMEM((rows, tokens), jnp.float32),
            pltpu.VMEM((rows, q_cols), jnp.bfloat16),
            pltpu.VMEM((chunks, tp // 2, rows, width), jnp.float32),
            pltpu.VMEM((chunks, tp - 1, rows, width), jnp.bfloat16),
            pltpu.VMEM((chunks, tp - 1, rows, width), jnp.bfloat16),
            pltpu.VMEM((n_ctx, 8, 128), jnp.float32),
            pltpu.VMEM((bits, 8, 128), jnp.float32),
            pltpu.VMEM((bits, 8, 128), jnp.float32),
            dma((3,)),
            dma((chunks, tp)),
            dma((2, n_ctx, 2)),
            dma((2, n_ctx, 2)),
            dma((chunks, tp - 1)),
            dma((chunks, tp - 1)),
            dma((n_ctx,)),
            dma((n_ctx,)),
            dma((bits,)),
            dma((bits,)),
        ],
        compiler_params=pltpu.CompilerParams(collective_id=0, has_side_effects=True),
    )(span_order, query_states, key_states, value_states, out_weight)
    return projected, z_loss.reshape(())


def solution(mesh):
    return jax.shard_map(
        functools.partial(on_device, mesh.shape["ctx"], mesh.shape["tp"]),
        mesh=mesh,
        in_specs=(P("ctx", "tp"), P("ctx", None), P("ctx", None), P("tp", None), P()),
        out_specs=(P("ctx", "tp"), P()),
        check_vma=False,
    )
```

time: 145 us -> 58.5 us (0.40)
  blocking collectives: 71 us -> 0 us
  Pallas kernels: 0 us -> 54.1 us
  waiting for transfers between devices: 31 us -> 0 us
  matrix products: 16 us -> 0 us
  between operations: 15.9 us -> 2.34 us
  other arithmetic: 7.33 us -> 0 us
    pallas_call x0 -> x1, Pallas kernels: none -> 54.1 us  [on_device(): pl.pallas_call(functools.partial(kernel, n_ctx, tp, heads, chunks, QH * t...]
    psum x1 -> x0, blocking collectives: 40.9 us -> none  [on_device(): squares_total = lax.psum(jnp.sum(log_norm * log_norm), ('ctx', 'tp'))]
    reduce_scatter x1 -> x0, waiting for transfers between devices: 31 us -> none  [on_device(): lax.psum_scatter(lax.dot_general(out_weight, attended, (((0,), (1,)), (()...]
    all_gather x2 -> x0, blocking collectives: 30.1 us -> none  [the longest x1 15.7 us: on_device(): value_piece = lax.all_gather(own_values, 'ctx', axis=0, tiled=True)]
    dot_general x3 -> x0, matrix products: 16 us -> none  [the longest x1 12.5 us: on_device(): lax.dot_general(out_weight, attended, (((0,), (1,)), ((), ())), preferred...]
    reduce_sum x4 -> x0, other arithmetic: 4.49 us -> none  [the longest x1 2.4 us: absorb(): normalizer = jnp.sum(exp_terms, axis=1)]
    convert_element_type x2 -> x0, other arithmetic: 2.8 us -> none  [the longest x1 2.09 us: on_device(): projected = jnp.transpose(summed).astype(jnp.bfloat16)]
  transfers between devices with their start and end apart: 1 -> 0, of which waited for: 1 -> 0; matrix products, arithmetic and copies ran while one was open for 0% -> 0% of each run, Pallas kernels for 0% -> 0%
where the time goes in v1:
time: 58.5 us; the launch traced here: 58.3 us
  Pallas kernels  54.1 us (92%)
  between operations  2.34 us (4%)
  local copies, waits for them, and re-layouts  1.87 us (3%)
    pallas_call x1, Pallas kernels, on_device(): pl.pallas_call(functools.partial(kernel, n_ctx, tp, heads, chunks, QH * t...  54.1 us
    unnamed x1, local copies, waits for them, and re-layouts  1.87 us

profile of v1, /device:TPU:0, one launch (start us, length us, event | category | flops | bytes accessed | tf_op | source)
XLA Modules:
  0.0 58.3 jit_solution(10578807681035105363)
XLA Ops:
  0.6 54.1 %shard_map.68 = (bf16[256,1024]{1,0:T(8,128)(2,1)}, f32[1,1]{1,0:T(1,128)}) custom-call(s32[8]{0:T(128)} %so_ref.1, bf16[256,1024]{1,0:T(8,128)(2,1)} %q_hbm.1, bf16[256,1024]{1,0:T(8,128)(2,1)} %k_hbm.1, bf16[256,1024]{1,0:T(8,128)(2,1)} %v_hbm.1, bf16[1024,8192]{1,0:T(8,128)(2,1)} %w_hbm.1), custom_call_target="tpu_custom_call" | custom-call | tf_op jit(solution)/shard_map/pallas_call | solution.py:267
  54.7 1.9 %copy.9 = bf16[256,1024]{1,0:T(8,128)(2,1)} copy(bf16[256,1024]{1,0:T(8,128)(2,1)} %get-tuple-element.8) | data formatting | bytes 1048576

commit v2 on v1

--- a/solution.py
+++ b/solution.py
@@ -48,7 +48,7 @@
     bits = tp.bit_length() - 1
     rows = qbuf.shape[0]
     span_rows = rows // 2
-    width = wbuf.shape[-1]
+    width = sbuf.shape[-1]
     cols = width * chunks
     tbit = [lax.rem(lax.div(t, 1 << b), 2) for b in range(bits)]
 
@@ -81,10 +81,12 @@
     w_in = {}
     for c in range(chunks):
         _, _, sends, keeps = plans[c]
-        for e in sends[0] + keeps[0]:
+        for place, e in enumerate(sends[0] + keeps[0]):
             start = pl.multiple_of(owner(e) * cols + c * width, width)
             w_in[c, e] = pltpu.make_async_copy(
-                w_hbm.at[:, pl.ds(start, width)], wbuf.at[c, e], w_sem.at[c, e]
+                w_hbm.at[:, pl.ds(start, width)],
+                wbuf.at[c, :, pl.ds(place * width, width)],
+                w_sem.at[c, e],
             )
             w_in[c, e].start()
     pl.semaphore_wait(barrier, n_ctx - 1 + bits)
@@ -133,7 +135,6 @@
                 k_pos <= q_pos, 0.0, neg_large
             )
     q_in.wait()
-
     for dist in range(1, n_ctx):
         for which in range(2):
             for d in range(2):
@@ -187,12 +188,19 @@
 
     def project(c):
         _, slots, sends, keeps = plans[c]
-        for e in sends[0]:
-            w_in[c, e].wait()
-            push(c, 0, e, jnp.dot(att[...], wbuf[c, e], preferred_element_type=jnp.float32))
-        for e in keeps[0]:
-            w_in[c, e].wait()
-            acc[c, slots[0, e]] = jnp.dot(att[...], wbuf[c, e], preferred_element_type=jnp.float32)
+        for group, blocks in enumerate((sends[0], keeps[0])):
+            for e in blocks:
+                w_in[c, e].wait()
+            span = len(blocks) * width
+            products = jnp.dot(
+                att[...], wbuf[c, :, group * span:(group + 1) * span], preferred_element_type=jnp.float32
+            )
+            for place, e in enumerate(blocks):
+                value = products[:, place * width:(place + 1) * width]
+                if group == 0:
+                    push(c, 0, e, value)
+                else:
+                    acc[c, slots[0, e]] = value
 
     def combine(c, stage):
         order, slots, sends, keeps = plans[c]
@@ -207,33 +215,40 @@
             else:
                 acc[c, slots[0, e]] = value
 
+    def zt_copy(b):
+        return pltpu.make_async_remote_copy(
+            src_ref=zsend.at[b], dst_ref=zrecv.at[b], send_sem=zt_send.at[b], recv_sem=zt_recv.at[b],
+            device_id=(z, partner(b)), device_id_type=MESH,
+        )
+
+    def z_steps():
+        for r in range(1, n_ctx):
+            zc_copy(r).wait_recv()
+        total = zctx[z]
+        for j in range(1, n_ctx):
+            total = total + zctx[lax.rem(z - j + n_ctx, n_ctx)]
+        for b in range(bits):
+            zsend[b] = total
+            zt_copy(b).start()
+            yield
+            zt_copy(b).wait_recv()
+            total = total + zrecv[b]
+        z_ref[...] = total[0:1, 0:1] * (z_coef / count)
+        yield
+
+    z_next = z_steps()
     for c in range(chunks):
         project(c)
         if c >= 1:
             combine(c - 1, 0)
+            next(z_next, None)
     combine(chunks - 1, 0)
-
-    for r in range(1, n_ctx):
-        zc_copy(r).wait_recv()
-    total = zctx[lax.rem(z, n_ctx)]
-    for j in range(1, n_ctx):
-        total = total + zctx[lax.rem(z - j + n_ctx, n_ctx)]
-
-    def zt_copy(b):
-        return pltpu.make_async_remote_copy(
-            src_ref=zsend.at[b], dst_ref=zrecv.at[b], send_sem=zt_send.at[b], recv_sem=zt_recv.at[b],
-            device_id=(z, partner(b)), device_id_type=MESH,
-        )
-
-    for b in range(bits):
-        zsend[b] = total
-        zt_copy(b).start()
-        if b + 1 < bits:
-            for c in range(chunks):
-                combine(c, b + 1)
-        zt_copy(b).wait_recv()
-        total = total + zrecv[b]
-    z_ref[...] = total[0:1, 0:1] * (z_coef / count)
+    for stage in range(1, bits):
+        for c in range(chunks):
+            combine(c, stage)
+            next(z_next, None)
+    for _ in z_next:
+        pass
 
     for which in range(2):
         for d in range(2):
@@ -276,7 +291,7 @@
             pltpu.VMEM((rows, q_cols), jnp.bfloat16),
             pltpu.VMEM((tokens, HD), jnp.bfloat16),
             pltpu.VMEM((tokens, HD), jnp.bfloat16),
-            pltpu.VMEM((chunks, tp, depth, width), jnp.bfloat16),
+            pltpu.VMEM((chunks, depth, tp * width), jnp.bfloat16),
             pltpu.VMEM((rows, tokens), jnp.float32),
             pltpu.VMEM((rows, q_cols), jnp.bfloat16),
             pltpu.VMEM((chunks, tp // 2, rows, width), jnp.float32),

time: 58.5 us -> 52 us (0.89)
  Pallas kernels: 54.1 us -> 47.6 us
    pallas_call x1, Pallas kernels: 54.1 us -> 47.6 us  [on_device(): pl.pallas_call(functools.partial(kernel, n_ctx, tp, heads, chunks, QH * t...]
where the time goes in v2:
time: 52 us; the launch traced here: 51.8 us
  Pallas kernels  47.6 us (92%)
  between operations  2.34 us (4%)
  local copies, waits for them, and re-layouts  1.87 us (4%)
    pallas_call x1, Pallas kernels, on_device(): pl.pallas_call(functools.partial(kernel, n_ctx, tp, heads, chunks, QH * t...  47.6 us
    unnamed x1, local copies, waits for them, and re-layouts  1.87 us

profile of v2, /device:TPU:0, one launch (start us, length us, event | category | flops | bytes accessed | tf_op | source)
XLA Modules:
  0.0 51.8 jit_solution(15533920898020385215)
XLA Ops:
  0.6 47.6 %shard_map.68 = (bf16[256,1024]{1,0:T(8,128)(2,1)}, f32[1,1]{1,0:T(1,128)}) custom-call(s32[8]{0:T(128)} %so_ref.1, bf16[256,1024]{1,0:T(8,128)(2,1)} %q_hbm.1, bf16[256,1024]{1,0:T(8,128)(2,1)} %k_hbm.1, bf16[256,1024]{1,0:T(8,128)(2,1)} %v_hbm.1, bf16[1024,8192]{1,0:T(8,128)(2,1)} %w_hbm.1), custom_call_target="tpu_custom_call" | custom-call | tf_op jit(solution)/shard_map/pallas_call | solution.py:282
  48.2 1.9 %copy.9 = bf16[256,1024]{1,0:T(8,128)(2,1)} copy(bf16[256,1024]{1,0:T(8,128)(2,1)} %get-tuple-element.8) | data formatting | bytes 1048576
